TPU v7x, 32 devices: a whole 2x2x4 slice. The times are simulated.
32 devices in a mesh: grp: 2 (over x), seq: 16 (over z, y, core).
Axes of the slice: x: 2, y: 2, z: 4, core: 2. Of those that a mesh axis runs over, the one named last changes fastest.
Arguments:
- queries: bfloat16 [512, 4096], P(('grp', 'seq')), parts along dimension 0, may hold values from -36 to 36
- new_keys: bfloat16 [512, 1024], P(('grp', 'seq')), parts along dimension 0, may hold values from -24 to 24
- new_values: bfloat16 [512, 1024], P(('grp', 'seq')), parts along dimension 0, may hold values from -12 to 12
- suffix_keys: bfloat16 [512, 256, 1024], P(('grp', 'seq')), parts along dimension 0, may hold values from -18 to 18
- suffix_values: bfloat16 [512, 256, 1024], P(('grp', 'seq')), parts along dimension 0, may hold values from -12 to 12
- suffix_lens: int32 [512], P(('grp', 'seq')), parts along dimension 0, may hold values from 1 to 256, 32768 in all
- prefix_keys: bfloat16 [2048, 16, 1024], P(('grp', 'seq')), parts along dimension 0, may hold values from -12 to 12
- prefix_values: bfloat16 [2048, 16, 1024], P(('grp', 'seq')), parts along dimension 0, may hold values from -12 to 12
- page_table: int32 [4, 512], P('grp'), parts along dimension 0, may hold values from 0 to 1023, as said below
- prefix_id: int32 [512], P('grp'), parts along dimension 0, may hold values from 0 to 1
Outputs:
- attn_out: bfloat16 [512, 4096], P(('grp', 'seq')), parts along dimension 0
There are 2 independent parts, one for each index of `grp`. A program takes and returns all parts, laid end to end along the dimension named above; each array names one. Nothing has to cross between parts.
Inputs may be any that keep to these rules, and one draw needn't show every extreme that they name: `page_table`: every page id 0 to 1023 stands exactly once in the table. Each run of 64 page ids that starts at a multiple of 64 holds at least one page of every prefix.
All inputs are finite; a program needn't handle non-finite values. No bound on the sum of `suffix_lens` on one device may be relied on, other than what follows from the above.
Results may differ from a plain program's by a relative error of at most 0.005.
Values may be sent and summed in bfloat16 or wider, within the bound.
A program may use at most 192 MiB of HBM per device.

v0:
```python
import functools
import math

import jax
import jax.numpy as jnp
from jax import lax
from jax.experimental import pallas as pl
from jax.experimental.pallas import tpu as pltpu
from jax.sharding import PartitionSpec as P

H = 32
KV = 8
HD = 128
NPREF = 2
G = H // KV
MASKED = -1e30
SCALE2 = math.log2(math.e) / math.sqrt(HD)
NT = (((1,), (1,)), ((), ()))


def low_bit(m):
    return m & (-m)


def kernel(
    n,
    q_hbm, nk_ref, nv_ref, sk_hbm, sv_hbm, lens_ref, pk_hbm, pv_hbm, label_ref, onehot_ref,
    out_ref,
    qs, sk, sv, pk, pv, part, lse, recv_o, recv_l, eg, q_rows, home_o, home_l,
    in_sem, suf_sem, ag_send, ag_recv, o_send, o_recv, l_send, l_recv,
):
    rows = q_hbm.shape[0]
    slots = sk.shape[1]
    me = lax.axis_index("seq")

    def flip(bit):
        return me + bit * (1 - 2 * ((me // bit) % 2))

    def xor(m):
        index = me
        bit = 1
        while bit < n:
            if m & bit:
                index = index + bit * (1 - 2 * ((me // bit) % 2))
            bit *= 2
        return index

    bits = [1 << i for i in range(n.bit_length() - 1)]

    q_copy = pltpu.make_async_copy(q_hbm, qs.at[0], in_sem.at[0])
    q_copy.start()
    for b in range(rows):
        pltpu.make_async_copy(sk_hbm.at[b], sk.at[b], suf_sem.at[0, b]).start()
        pltpu.make_async_copy(sv_hbm.at[b], sv.at[b], suf_sem.at[1, b]).start()
    k_copy = pltpu.make_async_copy(pk_hbm, pk, in_sem.at[1])
    v_copy = pltpu.make_async_copy(pv_hbm, pv, in_sem.at[2])
    k_copy.start()
    v_copy.start()

    barrier = pltpu.get_barrier_semaphore()
    for bit in bits:
        pl.semaphore_signal(
            barrier, inc=1, device_id={"seq": flip(bit)},
            device_id_type=pl.DeviceIdType.MESH,
        )
    pl.semaphore_wait(barrier, len(bits))
    q_copy.wait()

    def gather_copy(m):
        bit = low_bit(m)
        return pltpu.make_async_remote_copy(
            src_ref=qs.at[m ^ bit], dst_ref=qs.at[m],
            send_sem=ag_send.at[m], recv_sem=ag_recv.at[m],
            device_id={"seq": flip(bit)}, device_id_type=pl.DeviceIdType.MESH,
        )

    def forward(m):
        limit = n if m == 0 else low_bit(m)
        for bit in reversed(bits):
            if bit < limit:
                gather_copy(m + bit).start()

    arrived = set([0])

    def arrive(m):
        if m not in arrived:
            arrived.add(m)
            arrive(m ^ low_bit(m))
            gather_copy(m).wait_recv()
            forward(m)

    forward(0)

    for h in range(H):
        q_rows[pl.ds(h, rows, stride=H), :] = qs[0, :, h * HD:(h + 1) * HD].astype(jnp.float32)

    row_head = lax.broadcasted_iota(jnp.int32, (H, HD), 0) // G
    slot_iota = lax.broadcasted_iota(jnp.int32, (H, slots), 1)
    new_iota = lax.broadcasted_iota(jnp.int32, (H, rows), 1)

    def suffix(b, carry):
        pltpu.make_async_copy(sk_hbm.at[b], sk.at[b], suf_sem.at[0, b]).wait()
        pltpu.make_async_copy(sv_hbm.at[b], sv.at[b], suf_sem.at[1, b]).wait()
        q = q_rows[pl.ds(b * H, H), :]
        wide = jnp.concatenate(
            [jnp.where(row_head == k, q, 0.0) for k in range(KV)], axis=1
        ).astype(jnp.bfloat16)
        s = lax.dot_general(wide, sk[b], NT, preferred_element_type=jnp.float32)
        s = jnp.where(slot_iota < lens_ref[b], s, MASKED)
        sn = lax.dot_general(wide, nk_ref[...], NT, preferred_element_type=jnp.float32)
        sn = jnp.where(new_iota == b, sn, MASKED)
        peak = jnp.maximum(
            jnp.max(s, axis=1, keepdims=True), jnp.max(sn, axis=1, keepdims=True)
        )
        p = jnp.exp2((s - peak) * SCALE2)
        pn = jnp.exp2((sn - peak) * SCALE2)
        mass = jnp.sum(p, axis=1, keepdims=True) + jnp.sum(pn, axis=1, keepdims=True)
        o = jnp.dot(p.astype(jnp.bfloat16), sv[b], preferred_element_type=jnp.float32)
        o = o + jnp.dot(pn.astype(jnp.bfloat16), nv_ref[...], preferred_element_type=jnp.float32)
        own = jnp.zeros((H, HD), jnp.float32)
        for k in range(KV):
            own = own + jnp.where(row_head == k, o[:, k * HD:(k + 1) * HD], 0.0)
        home_o[pl.ds(b * H, H), :] = own / mass
        home_l[pl.ds(b * H, H), :] = jnp.broadcast_to(
            peak * SCALE2 + jnp.log2(mass), (H, HD)
        )
        return carry

    arrival = sorted(range(1, n), key=lambda m: (bin(m).count("1"), -m if m & (m - 1) else m))
    even = [m for m in arrival if m % 2 == 0]
    segments = 8
    cut = [rows * i // segments for i in range(segments + 1)]
    share = [len(even) * i // segments for i in range(segments + 1)]
    for i in range(segments):
        lax.fori_loop(cut[i], cut[i + 1], suffix, 0)
        for m in even[share[i]:share[i + 1]]:
            arrive(m)

    k_copy.wait()
    v_copy.wait()
    lane = lax.broadcasted_iota(jnp.int32, (rows, HD), 1)
    tokens = pk.shape[0]

    def compute(blocks, first, last):
        def head(k, carry):
            base = pl.multiple_of(k * (G * HD), G * HD)
            cols = pl.ds(pl.multiple_of(k * HD, HD), HD)
            q = jnp.concatenate(
                [qs[m, :, pl.ds(base + g * HD, HD)] for m in blocks for g in range(G)], axis=0
            )
            qx = jnp.concatenate([q, eg[...]], axis=1)
            kx = jnp.concatenate([pk[:, cols], label_ref[...]], axis=1)
            s = lax.dot_general(qx, kx, NT, preferred_element_type=jnp.float32)
            peak = jnp.max(s, axis=1, keepdims=True)
            p = jnp.exp2((s - peak) * SCALE2).astype(jnp.bfloat16)
            vx = jnp.concatenate(
                [pv[:, cols], jnp.ones((tokens, HD), jnp.bfloat16)], axis=1
            )
            o = jnp.dot(p, vx, preferred_element_type=jnp.float32)
            mass = o[:, HD:]
            res = (o[:, :HD] / mass).astype(jnp.bfloat16)
            level = peak * SCALE2 + jnp.log2(mass)
            for i, m in enumerate(blocks):
                total = lse[m]
                for g in range(G):
                    at = (i * G + g) * rows
                    part[m, :, pl.ds(base + g * HD, HD)] = res[at:at + rows]
                    total = jnp.where(lane == k * G + g, level[at:at + rows], total)
                lse[m] = total
            return carry

        lax.fori_loop(first, last, head, 0, unroll=4)

    def partner_copies(m):
        where = {"seq": flip(low_bit(m))}
        return [
            pltpu.make_async_remote_copy(
                src_ref=src.at[m], dst_ref=dst.at[m], send_sem=s.at[m], recv_sem=r.at[m],
                device_id=where, device_id_type=pl.DeviceIdType.MESH,
            )
            for src, dst, s, r in ((part, recv_o, o_send, o_recv), (lse, recv_l, l_send, l_recv))
        ]

    def send(m):
        for copy in partner_copies(m):
            copy.start()

    def pick(w, h):
        return jnp.sum(jnp.where(lane == h, w, 0.0), axis=1, keepdims=True)

    def blend(a, b):
        top = jnp.maximum(a, b)
        return 1.0 / (1.0 + jnp.exp2(b - a)), top + jnp.log2(1.0 + jnp.exp2(-jnp.abs(a - b)))

    def merge(m, child):
        for copy in partner_copies(child):
            copy.wait_recv()
        w, level = blend(recv_l[child], lse[m])
        lse[m] = level

        def step(k, carry):
            base = pl.multiple_of(k * (G * HD), G * HD)
            for g in range(G):
                at = pl.ds(base + g * HD, HD)
                a = recv_o[child, :, at].astype(jnp.float32)
                b = part[m, :, at].astype(jnp.float32)
                part[m, :, at] = (b + (a - b) * pick(w, k * G + g)).astype(jnp.bfloat16)
            return carry

        lax.fori_loop(0, KV, step, 0, unroll=4)

    pairs = [m for m in range(0, n, 2)]
    pairs.sort(key=lambda m: (low_bit(m) != 2, -m))
    groups = [pairs[i:i + 2] for i in range(0, len(pairs), 2)]

    def settle(group):
        for m in group:
            if m == 0:
                continue
            bit = 1
            while bit < low_bit(m):
                merge(m, m + bit)
                bit *= 2
            send(m)

    waiting, late = [], []
    for group in groups:
        blocks = [m + odd for m in group for odd in (1, 0)]
        for m in blocks:
            arrive(m)
            lse[m] = jnp.zeros((rows, HD), jnp.float32)
        for i, m in enumerate(blocks):
            code = onehot_ref[xor(m)]
            for g in range(G):
                at = (i * G + g) * rows
                eg[at:at + rows] = code
        half = KV // 2
        compute(blocks, 0, half)
        settle([m for m in waiting if low_bit(m) <= 4])
        late += [m for m in waiting if low_bit(m) > 4]
        compute(blocks, half, KV)
        for m in blocks:
            if m % 2:
                send(m)
        waiting = group
    settle(sorted(late + waiting, key=low_bit))

    for bit in bits[:-1]:
        merge(0, bit)
    last = bits[-1]
    for copy in partner_copies(last):
        copy.wait_recv()
    w, level = blend(recv_l[last], lse[0])

    def finish(k, carry):
        base = pl.multiple_of(k * (G * HD), G * HD)
        for g in range(G):
            h = k * G + g
            at = pl.ds(base + g * HD, HD)
            a = recv_o[last, :, at].astype(jnp.float32)
            b = part[0, :, at].astype(jnp.float32)
            x = b + (a - b) * pick(w, h)
            mine = pl.ds(h, rows, stride=H)
            home = home_o[mine, :]
            w_home = 1.0 / (1.0 + jnp.exp2(pick(level, h) - home_l[mine, :]))
            out_ref[:, at] = (x + (home - x) * w_home).astype(jnp.bfloat16)
        return carry

    lax.fori_loop(0, KV, finish, 0, unroll=2)
    for m in range(1, n):
        gather_copy(m).wait_send()
        for copy in partner_copies(m):
            copy.wait_send()


def local(
    queries, new_keys, new_values, suffix_keys, suffix_values, suffix_lens,
    prefix_keys, prefix_values, page_table, prefix_id,
):
    n = lax.axis_size("seq")
    rows = queries.shape[0]
    slots = suffix_keys.shape[1]
    pages, page, width = prefix_keys.shape
    tokens = pages * page
    ids = lax.axis_index("seq") * pages + jnp.arange(pages, dtype=jnp.int32)
    hits = jnp.any(page_table[:, :, None] == ids[None, None, :], axis=1)
    prefixes = jnp.arange(NPREF, dtype=jnp.int32)
    label = jnp.sum(hits.astype(jnp.int32) * prefixes[:, None], axis=0)
    lanes = jnp.arange(HD, dtype=jnp.int32)
    barred = (lanes[None, :] < NPREF) & (lanes[None, :] != label[:, None])
    label_cols = jnp.where(barred, MASKED, 0.0).astype(jnp.bfloat16)
    label_cols = jnp.broadcast_to(label_cols[:, None, :], (pages, page, HD)).reshape(tokens, HD)
    onehot = (prefix_id.reshape(n, rows, 1) == lanes).astype(jnp.bfloat16)
    vmem = pl.BlockSpec(memory_space=pltpu.VMEM)
    hbm = pl.BlockSpec(memory_space=pl.ANY)
    smem = pl.BlockSpec(memory_space=pltpu.SMEM)
    bf16, f32 = jnp.bfloat16, jnp.float32
    dma = pltpu.SemaphoreType.DMA
    return pl.pallas_call(
        functools.partial(kernel, n),
        out_shape=jax.ShapeDtypeStruct((rows, H * HD), bf16),
        in_specs=[hbm, vmem, vmem, hbm, hbm, smem, hbm, hbm, vmem, vmem],
        out_specs=vmem,
        scratch_shapes=[
            pltpu.VMEM((n, rows, H * HD), bf16),
            pltpu.VMEM((rows, slots, width), bf16),
            pltpu.VMEM((rows, slots, width), bf16),
            pltpu.VMEM((tokens, width), bf16),
            pltpu.VMEM((tokens, width), bf16),
            pltpu.VMEM((n, rows, H * HD), bf16),
            pltpu.VMEM((n, rows, HD), f32),
            pltpu.VMEM((n, rows, H * HD), bf16),
            pltpu.VMEM((n, rows, HD), f32),
            pltpu.VMEM((4 * G * rows, HD), bf16),
            pltpu.VMEM((rows * H, HD), f32),
            pltpu.VMEM((rows * H, HD), f32),
            pltpu.VMEM((rows * H, HD), f32),
            dma((3,)),
            dma((2, rows)),
            dma((n,)), dma((n,)), dma((n,)), dma((n,)), dma((n,)), dma((n,)),
        ],
        compiler_params=pltpu.CompilerParams(
            collective_id=0, has_side_effects=True, vmem_limit_bytes=64 * 1024 * 1024 - 65536,
        ),
        name="step",
    )(
        queries, new_keys, new_values, suffix_keys, suffix_values, suffix_lens,
        prefix_keys.reshape(tokens, width), prefix_values.reshape(tokens, width),
        label_cols, onehot,
    )


def solution(mesh):
    return jax.shard_map(
        local,
        mesh=mesh,
        in_specs=(
            P(("grp", "seq"), None),
            P(("grp", "seq"), None),
            P(("grp", "seq"), None),
            P(("grp", "seq"), None, None),
            P(("grp", "seq"), None, None),
            P(("grp", "seq")),
            P(("grp", "seq"), None, None),
            P(("grp", "seq"), None, None),
            P("grp", None),
            P("grp"),
        ),
        out_specs=P(("grp", "seq"), None),
        check_vma=False,
    )
```

profile of v0, /device:TPU:0, one launch (start us, length us, event | category | flops | bytes accessed | tf_op | source)
XLA Modules:
  0.0 64.2 jit_solution(3731072287703958707)
XLA Ops:
  0.0 0.9 %compare_reduce_fusion = pred[2,64]{1,0:T(4,128)(4,1)S(1)} fusion(s32[2,512]{1,0:T(2,128)} %param.18, s32[64]{0:T(128)S(1)} %iota_add_fusion), kind=kLoop, calls=%fused_computation | loop fusion | flops 130944 | bytes 4480 | tf_op jit(solution)/shard_map/reduce_or | solution.py:286
  0.9 0.8 %eq.31 = s32[16,16]{1,0:T(8,128)S(1)} reshape(s32[256]{0:T(256)} %param.19) | data formatting | bytes 2048 | tf_op jit(solution)/shard_map/eq | solution.py:293
  1.7 0.1 select_convert_fusion
  1.8 0.7 %fusion.onehot_ref = bf16[16,16,128]{2,1,0:T(8,128)(2,1)} fusion(s32[16,16]{1,0:T(8,128)S(1)} %eq.31), kind=kLoop, calls=%fused_computation.2 | loop fusion | flops 65536 | bytes 66560 | tf_op jit(solution)/shard_map/convert_element_type | solution.py:293
  2.5 0.7 %broadcast_in_dim.12 = bf16[64,16,128]{2,1,0:T(8,128)(2,1)} broadcast(bf16[64,128]{1,0:T(8,128)(2,1)S(1)} %select_convert_fusion), dimensions={0,2} | broadcast | bytes 278528 | tf_op jit(solution)/shard_map/broadcast_in_dim | solution.py:292
  3.2 59.4 %step.1 = bf16[16,4096]{1,0:T(8,128)(2,1)} custom-call(bf16[16,4096]{1,0:T(8,128)(2,1)} %q_hbm.1, bf16[16,1024]{1,0:T(8,128)(2,1)} %nk_ref.1, bf16[16,1024]{1,0:T(8,128)(2,1)} %nv_ref.1, bf16[16,256,1024]{2,1,0:T(8,128)(2,1)} %sk_hbm.1, bf16[16,256,1024]{2,1,0:T(8,128)(2,1)} %sv_hbm.1, s32[16]{0:T(128)} %lens_ref.1, bf16[1024,1024]{1,0:T(8,128)(2,1)} %bitcast.3, ...), custom_call_target="tpu_custom_call" | custom-call | tf_op jit(solution)/shard_map/step/pallas_call | solution.py:299
  62.6 1.6 %copy.12 = bf16[16,4096]{1,0:T(8,128)(2,1)} copy(bf16[16,4096]{1,0:T(8,128)(2,1)} %step.1) | data formatting | bytes 262144
  (3 shorter events, 0.0 us)
where the time goes:
time: 64.3 us; the launch traced here: 64.2 us
  Pallas kernels  59.4 us (92%)
  local copies, waits for them, and re-layouts  3.05 us (5%)
  other arithmetic  1.72 us (3%)
    pallas_call x1, Pallas kernels, local(): pl.pallas_call(functools.partial(kernel, n), out_shape=jax.ShapeDtypeStru...  59.4 us
    unnamed x1, local copies, waits for them, and re-layouts  1.57 us

commit v1 on v0

v1 whole, which is shorter than its diff:
```python
import functools
import math

import jax
import jax.numpy as jnp
from jax import lax
from jax.experimental import pallas as pl
from jax.experimental.pallas import tpu as pltpu
from jax.sharding import PartitionSpec as P

H = 32
KV = 8
HD = 128
NPREF = 2
G = H // KV
HALF = KV // 2
MASKED = -1e30
SCALE2 = math.log2(math.e) / math.sqrt(HD)
NT = (((1,), (1,)), ((), ()))
MESH = pl.DeviceIdType.MESH


def low_bit(m):
    return m & (-m)


def kernel(
    n, page,
    q_hbm, nk_ref, nv_ref, sk_hbm, sv_hbm, lens_ref, pk_hbm, pv_hbm, table_ref, pid_ref,
    out_ref,
    q_own, qs, sk, sv, pk, pv, vt, label, onehot, scores,
    part, lse, near, near_l, far, far_l, fin, fin_l, got, got_l, cols, cols_got,
    q_rows, nk_rows, nv_rows, home_o, home_l,
    in_sem, suf_sem, kv_send, kv_recv, ag_send, ag_recv,
    o_send, o_recv, l_send, l_recv, f_send, f_recv,
):
    rows = q_hbm.shape[0]
    slots = sk.shape[1]
    tokens = pk_hbm.shape[0]
    wide_cols = H * HD // 2
    kv_cols = KV * HD // 2
    lanes = 2 * rows * G
    chips = n // 2
    me = lax.axis_index("seq")
    core = me % 2
    chip = me // 2
    other = 1 - core

    def chip_xor(m):
        index = chip
        bit = 1
        while bit < chips:
            if m & bit:
                index = index + bit * (1 - 2 * ((chip // bit) % 2))
            bit *= 2
        return index

    def dev(m, c):
        return chip_xor(m) * 2 + c

    bits = [1 << i for i in range(chips.bit_length() - 1)]
    evens = [m for m in range(2, chips, 2)]

    def q_half(h):
        return pl.ds(pl.multiple_of(h * wide_cols, wide_cols), wide_cols)

    def kv_half(h):
        return pl.ds(pl.multiple_of(h * kv_cols, kv_cols), kv_cols)

    def token_half(h):
        return pl.ds(pl.multiple_of(h * tokens, tokens), tokens)

    def remote(src, dst, send, recv, where):
        return pltpu.make_async_remote_copy(
            src_ref=src, dst_ref=dst, send_sem=send, recv_sem=recv,
            device_id={"seq": where}, device_id_type=MESH,
        )

    q_copy = pltpu.make_async_copy(q_hbm, q_own, in_sem.at[0])
    q_mine = pltpu.make_async_copy(q_hbm.at[:, q_half(core)], qs.at[0, core], in_sem.at[1])
    k_mine = pltpu.make_async_copy(
        pk_hbm.at[:, kv_half(core)], pk.at[token_half(core)], in_sem.at[2])
    v_mine = pltpu.make_async_copy(
        pv_hbm.at[:, kv_half(core)], pv.at[token_half(core)], in_sem.at[3])
    q_copy.start()
    q_mine.start()

    def suffix_copies(b):
        return (
            pltpu.make_async_copy(sk_hbm.at[b], sk.at[b], suf_sem.at[0, b]),
            pltpu.make_async_copy(sv_hbm.at[b], sv.at[b], suf_sem.at[1, b]),
        )

    barrier = pltpu.get_barrier_semaphore()
    peers = [dev(0, other)]
    for b in bits:
        peers += [dev(b, 0), dev(b, 1)]
    peers += [dev(m, core) for m in evens if m & (m - 1)]
    for peer in peers:
        pl.semaphore_signal(barrier, inc=1, device_id={"seq": peer}, device_id_type=MESH)
    for b in range(rows // 2):
        for copy in suffix_copies(b):
            copy.start()
    k_mine.start()
    v_mine.start()
    for b in range(rows // 2, rows):
        for copy in suffix_copies(b):
            copy.start()
    pl.semaphore_wait(barrier, len(peers))
    q_copy.wait()

    def own_copy(b, h):
        return remote(
            q_own.at[:, h * wide_cols:(h + 1) * wide_cols], qs.at[b, core],
            ag_send.at[b, h], ag_recv.at[b, core], dev(b, h))

    def forward_copy(m, s):
        return remote(
            qs.at[m ^ low_bit(m), s], qs.at[m, s],
            ag_send.at[m, s], ag_recv.at[m, s], dev(low_bit(m), core))

    partner_q = remote(
        q_own.at[:, q_half(other)], qs.at[0, core],
        ag_send.at[0, 0], ag_recv.at[0, 0], dev(0, other))
    partner_kv = [
        remote(src.at[:, kv_half(other)], dst.at[token_half(core)],
               kv_send.at[i], kv_recv.at[i], dev(0, other))
        for i, (src, dst) in enumerate(((pk_hbm, pk), (pv_hbm, pv)))
    ]

    for b in reversed(bits):
        for h in range(2):
            own_copy(b, h).start()
    partner_q.start()
    for copy in partner_kv:
        copy.start()

    arrived = set([0])

    def arrive(m):
        if m in arrived:
            return
        arrived.add(m)
        arrive(m ^ low_bit(m))
        for s in range(2):
            if m & (m - 1):
                forward_copy(m, s).wait_recv()
            else:
                remote(
                    q_own.at[:, 0:wide_cols], qs.at[m, s],
                    ag_send.at[m, s], ag_recv.at[m, s], dev(m, core)).wait_recv()
            for bit in reversed(bits):
                if bit < low_bit(m):
                    forward_copy(m + bit, s).start()

    lse[...] = jnp.zeros(lse.shape, jnp.float32)

    for h in range(H):
        at = pl.ds(h, rows, stride=H)
        k = h // G
        q_rows[at, :] = q_own[:, h * HD:(h + 1) * HD].astype(jnp.float32)
        nk_rows[at, :] = nk_ref[:, k * HD:(k + 1) * HD].astype(jnp.float32)
        nv_rows[at, :] = nv_ref[:, k * HD:(k + 1) * HD].astype(jnp.float32)

    row_head = lax.broadcasted_iota(jnp.int32, (H, HD), 0) // G
    slot_iota = lax.broadcasted_iota(jnp.int32, (H, slots), 1)

    def suffix_one(b):
        at = pl.ds(pl.multiple_of(b * H, H), H)
        q = q_rows[at, :]
        wide = jnp.concatenate(
            [jnp.where(row_head == k, q, 0.0) for k in range(KV)], axis=1
        ).astype(jnp.bfloat16)
        s = lax.dot_general(wide, sk[b], NT, preferred_element_type=jnp.float32)
        s = jnp.where(slot_iota < lens_ref[b], s, MASKED)
        sn = jnp.sum(q * nk_rows[at, :], axis=1, keepdims=True)
        peak = jnp.maximum(jnp.max(s, axis=1, keepdims=True), sn)
        p = jnp.exp2((s - peak) * SCALE2)
        pn = jnp.exp2((sn - peak) * SCALE2)
        mass = jnp.sum(p, axis=1, keepdims=True) + pn
        o = jnp.dot(p.astype(jnp.bfloat16), sv[b], preferred_element_type=jnp.float32)
        own = pn * nv_rows[at, :]
        for k in range(KV):
            own = own + jnp.where(row_head == k, o[:, k * HD:(k + 1) * HD], 0.0)
        home_o[at, :] = own / mass
        home_l[at, :] = jnp.broadcast_to(peak * SCALE2 + jnp.log2(mass), (H, HD))

    def suffix(first, last):
        for b in range(first, last):
            for copy in suffix_copies(b):
                copy.wait()
        for b in range(first, last):
            suffix_one(b)

    def prepare_labels():
        seqs = n * rows
        diag = (lax.broadcasted_iota(jnp.int32, (seqs, seqs), 0)
                == lax.broadcasted_iota(jnp.int32, (seqs, seqs), 1))
        pid = jnp.sum(jnp.where(diag, pid_ref[...].astype(jnp.float32), 0.0), axis=1, keepdims=True)
        lane = lax.broadcasted_iota(jnp.int32, (seqs, HD), 1).astype(jnp.float32)
        onehot[...] = jnp.where(lane == pid, 1.0, 0.0).astype(jnp.bfloat16)
        pages = 2 * tokens // page
        entries = table_ref.shape[1]
        ids = chip * pages + lax.broadcasted_iota(jnp.int32, (pages, entries), 0)
        page_lane = lax.broadcasted_iota(jnp.int32, (pages, HD), 1)
        bar = jnp.zeros((pages, HD), jnp.float32)
        for p in range(NPREF):
            hit = jnp.max(
                jnp.where(table_ref[p:p + 1, :] == ids, 1.0, 0.0), axis=1, keepdims=True)
            bar = jnp.where(page_lane == p, (1.0 - hit) * MASKED, bar)
        token = lax.broadcasted_iota(jnp.int32, (2 * tokens, pages), 0)
        first = lax.broadcasted_iota(jnp.int32, (2 * tokens, pages), 1) * page
        spread = jnp.where((token >= first) & (token < first + page), 1.0, 0.0)
        label[...] = jnp.dot(
            spread.astype(jnp.bfloat16), bar.astype(jnp.bfloat16),
            preferred_element_type=jnp.float32).astype(jnp.bfloat16)

    def prepare_values():
        v_mine.wait()
        partner_kv[1].wait_recv()
        step = 256
        for k in range(HALF):
            for t in range(0, 2 * tokens, step):
                vt[k, :HD, t:t + step] = pv[t:t + step, k * HD:(k + 1) * HD].T
            vt[k, HD:, :] = jnp.ones((vt.shape[1] - HD, 2 * tokens), jnp.bfloat16)

    def compute(blocks, j):
        parts = [(m, s) for m in blocks for s in range(2)]
        code = jnp.concatenate(
            [onehot[pl.ds(pl.multiple_of(dev(m, s) * rows, rows), rows), :]
             for m, s in parts for g in range(G)], axis=0)
        for i in range(HALF // 2):
            k = j * (HALF // 2) + i
            buf = scores.at[i]
            q = jnp.concatenate(
                [qs[m, s, :, (k * G + g) * HD:(k * G + g + 1) * HD]
                 for m, s in parts for g in range(G)], axis=0)
            qx = jnp.concatenate([q, code], axis=1)
            step = 512
            peak = None
            for t in range(0, 2 * tokens, step):
                kx = jnp.concatenate(
                    [pk[t:t + step, k * HD:(k + 1) * HD], label[t:t + step, :]], axis=1)
                s = lax.dot_general(kx, qx, NT, preferred_element_type=jnp.float32)
                buf[t:t + step, :] = s
                top = jnp.max(s, axis=0, keepdims=True)
                peak = top if peak is None else jnp.maximum(peak, top)
            o = None
            for t in range(0, 2 * tokens, step):
                p = jnp.exp2((buf[t:t + step, :] - peak) * SCALE2).astype(jnp.bfloat16)
                d = jnp.dot(vt[k, :, t:t + step], p, preferred_element_type=jnp.float32)
                o = d if o is None else o + d
            mass = o[HD:HD + 1, :]
            res = (o[:HD, :] * (1.0 / mass)).astype(jnp.bfloat16)
            level = peak * SCALE2 + jnp.log2(mass)
            for x, m in enumerate(blocks):
                part[m, j, i * HD:(i + 1) * HD, :] = res[:, x * lanes:(x + 1) * lanes]
                lse[m, j, i:i + 1, :] = level[:, x * lanes:(x + 1) * lanes]

    def near_copies(m, j):
        return [
            remote(part.at[m, j], near.at[m, j], o_send.at[m, j], o_recv.at[m, j], dev(1, core)),
            remote(lse.at[m, j], near_l.at[m, j], l_send.at[m, j], l_recv.at[m, j], dev(1, core)),
        ]

    def far_copies(m, j):
        return [
            remote(part.at[m, j], far.at[m, j], o_send.at[m, j], o_recv.at[m, j], dev(m, core)),
            remote(lse.at[m, j], far_l.at[m, j], l_send.at[m, j], l_recv.at[m, j], dev(m, core)),
        ]

    def send(copies):
        for copy in copies:
            copy.start()

    def merge(m, j, copies, src, src_l):
        for copy in copies:
            copy.wait_recv()
        for i in range(HALF // 2):
            la, lb = src_l[j, i:i + 1, :], lse[m, j, i:i + 1, :]
            w = 1.0 / (1.0 + jnp.exp2(lb - la))
            lse[m, j, i:i + 1, :] = jnp.maximum(la, lb) + jnp.log2(1.0 + jnp.exp2(-jnp.abs(la - lb)))
            at = slice(i * HD, (i + 1) * HD)
            a = src[j, at, :].astype(jnp.float32)
            b = part[m, j, at, :].astype(jnp.float32)
            part[m, j, at, :] = (b + (a - b) * w).astype(jnp.bfloat16)

    def merge_near(m, j):
        merge(m, j, near_copies(m + 1, j), near.at[m + 1], near_l.at[m + 1])

    def merge_far(m, j):
        merge(0, j, far_copies(m, j), far.at[m], far_l.at[m])

    def settle(m, j):
        merge_near(m, j)
        send(far_copies(m, j))

    quarter = max(1, rows // 4)
    cuts = [min(rows, quarter * i) for i in range(5)]
    arrive_after = {0: [], 1: [], 2: [], 3: []}
    by_count = sorted(evens, key=lambda m: (bin(m).count("1"), -m))
    for i, m in enumerate(by_count):
        arrive_after[min(3, 1 + i)].append(m)
    prepare_labels()
    for i in range(4):
        suffix(cuts[i], cuts[i + 1])
        for m in arrive_after[i]:
            arrive(m)
    k_mine.wait()
    partner_kv[0].wait_recv()
    q_mine.wait()
    remote(q_own.at[:, 0:wide_cols], qs.at[0, other],
           ag_send.at[0, 0], ag_recv.at[0, 0], dev(0, other)).wait_recv()
    prepare_values()

    order = by_count[::-1] if False else sorted(evens, key=lambda m: (bin(m).count("1"), m))
    waiting = []
    for m in order + [0]:
        arrive(m)
        arrive(m + 1)
        for j in range(2):
            compute([m, m + 1], j)
            send(near_copies(m + 1, j))
            for w in waiting:
                settle(w, j)
        waiting = [m] if m else []
    for j in range(2):
        merge_near(0, j)
    for m in order:
        for j in range(2):
            merge_far(m, j)

    def column(src):
        return jnp.concatenate([src] * (HD // src.shape[0]), axis=0).T

    for j in range(2):
        for i in range(HALF // 2):
            k = j * (HALF // 2) + i
            fin[k] = part[0, j, i * HD:(i + 1) * HD, :].astype(jnp.float32).T.astype(jnp.bfloat16)
    mine = rows * G
    give = remote(
        fin.at[:, pl.ds(pl.multiple_of(other * mine, mine), mine), :], got,
        f_send.at[0], f_recv.at[0], dev(0, other))
    give_l = remote(lse.at[0], got_l, f_send.at[1], f_recv.at[1], dev(0, other))
    give.start()
    give_l.start()

    def finish(half, levels, value):
        for k in range(HALF):
            j, i = k // (HALF // 2), k % (HALF // 2)
            for g in range(G):
                head = half * (HALF * G) + k * G + g
                level = levels[j, pl.ds(pl.multiple_of(core * mine + g * rows, rows), rows), i:i + 1]
                x = value(k, g).astype(jnp.float32)
                at = pl.ds(head, rows, stride=H)
                home = home_o[at, :]
                w = 1.0 / (1.0 + jnp.exp2(level - home_l[at, :]))
                out_ref[:, pl.ds(pl.multiple_of(head * HD, HD), HD)] = (
                    x + (home - x) * w).astype(jnp.bfloat16)

    for j in range(2):
        cols[j] = column(lse[0, j])
    finish(core, cols, lambda k, g: fin[
        k, pl.ds(pl.multiple_of(core * mine + g * rows, rows), rows), :])
    give.wait_recv()
    give_l.wait_recv()
    for j in range(2):
        cols_got[j] = column(got_l[j])
    finish(other, cols_got, lambda k, g: got[k, g * rows:(g + 1) * rows, :])

    for b in bits:
        for h in range(2):
            own_copy(b, h).wait_send()
    for m in range(1, chips):
        if m & (m - 1):
            for s in range(2):
                forward_copy(m, s).wait_send()
    partner_q.wait_send()
    for copy in partner_kv:
        copy.wait_send()
    for m in range(1, chips):
        for j in range(2):
            for copy in (near_copies(m, j) if m % 2 else far_copies(m, j)):
                copy.wait_send()
    give.wait_send()
    give_l.wait_send()


def local(
    queries, new_keys, new_values, suffix_keys, suffix_values, suffix_lens,
    prefix_keys, prefix_values, page_table, prefix_id,
):
    n = lax.axis_size("seq")
    chips = n // 2
    rows = queries.shape[0]
    slots = suffix_keys.shape[1]
    pages, page, width = prefix_keys.shape
    tokens = pages * page
    vmem = pl.BlockSpec(memory_space=pltpu.VMEM)
    hbm = pl.BlockSpec(memory_space=pl.ANY)
    smem = pl.BlockSpec(memory_space=pltpu.SMEM)
    bf16, f32 = jnp.bfloat16, jnp.float32
    dma = pltpu.SemaphoreType.DMA
    lanes = 2 * rows * G
    deep = HALF // 2 * HD
    return pl.pallas_call(
        functools.partial(kernel, n, page),
        out_shape=jax.ShapeDtypeStruct((rows, H * HD), bf16),
        in_specs=[hbm, vmem, vmem, hbm, hbm, smem, hbm, hbm, vmem, vmem],
        out_specs=vmem,
        scratch_shapes=[
            pltpu.VMEM((rows, H * HD), bf16),
            pltpu.VMEM((chips, 2, rows, H * HD // 2), bf16),
            pltpu.VMEM((rows, slots, width), bf16),
            pltpu.VMEM((rows, slots, width), bf16),
            pltpu.VMEM((2 * tokens, width // 2), bf16),
            pltpu.VMEM((2 * tokens, width // 2), bf16),
            pltpu.VMEM((HALF, HD + 16, 2 * tokens), bf16),
            pltpu.VMEM((2 * tokens, HD), bf16),
            pltpu.VMEM((n * rows, HD), bf16),
            pltpu.VMEM((HALF // 2, 2 * tokens, 2 * lanes), f32),
            pltpu.VMEM((chips, 2, deep, lanes), bf16),
            pltpu.VMEM((chips, 2, 8, lanes), f32),
            pltpu.VMEM((chips, 2, deep, lanes), bf16),
            pltpu.VMEM((chips, 2, 8, lanes), f32),
            pltpu.VMEM((chips, 2, deep, lanes), bf16),
            pltpu.VMEM((chips, 2, 8, lanes), f32),
            pltpu.VMEM((HALF, lanes, HD), bf16),
            pltpu.VMEM((2, 8, lanes), f32),
            pltpu.VMEM((HALF, rows * G, HD), bf16),
            pltpu.VMEM((2, 8, lanes), f32),
            pltpu.VMEM((2, lanes, HD), f32),
            pltpu.VMEM((2, lanes, HD), f32),
            pltpu.VMEM((rows * H, HD), f32),
            pltpu.VMEM((rows * H, HD), f32),
            pltpu.VMEM((rows * H, HD), f32),
            pltpu.VMEM((rows * H, HD), f32),
            pltpu.VMEM((rows * H, HD), f32),
            dma((4,)),
            dma((2, rows)),
            dma((2,)), dma((2,)),
            dma((chips, 2)), dma((chips, 2)),
            dma((chips, 2)), dma((chips, 2)), dma((chips, 2)), dma((chips, 2)),
            dma((2,)), dma((2,)),
        ],
        compiler_params=pltpu.CompilerParams(
            collective_id=0, has_side_effects=True, vmem_limit_bytes=64 * 1024 * 1024 - 65536,
        ),
        name="step",
    )(
        queries, new_keys, new_values, suffix_keys, suffix_values, suffix_lens,
        prefix_keys.reshape(tokens, width), prefix_values.reshape(tokens, width),
        page_table, prefix_id.reshape(1, n * rows),
    )


def solution(mesh):
    return jax.shard_map(
        local,
        mesh=mesh,
        in_specs=(
            P(("grp", "seq"), None),
            P(("grp", "seq"), None),
            P(("grp", "seq"), None),
            P(("grp", "seq"), None, None),
            P(("grp", "seq"), None, None),
            P(("grp", "seq")),
            P(("grp", "seq"), None, None),
            P(("grp", "seq"), None, None),
            P("grp", None),
            P("grp"),
        ),
        out_specs=P(("grp", "seq"), None),
        check_vma=False,
    )
```

time: 64.3 us -> 49.5 us (0.77)
  Pallas kernels: 59.4 us -> 47.5 us
  other arithmetic: 1.72 us -> 0 us
  local copies, waits for them, and re-layouts: 3.05 us -> 1.57 us
    pallas_call x1, Pallas kernels: 59.4 us -> 47.5 us  [local(): pl.pallas_call(functools.partial(kernel, n, page), out_shape=jax.ShapeDty...]
    reduce_or x1 -> x0, other arithmetic: 0.88 us -> none  [local(): hits = jnp.any(page_table[:, :, None] == ids[None, None, :], axis=1)]
    convert_element_type x2 -> x0, other arithmetic: 0.81 us -> none  [the longest x1 0.73 us: local(): onehot = (prefix_id.reshape(n, rows, 1) == lanes).astype(jnp.bfloat16)]
    eq x1 -> x0, local copies, waits for them, and re-layouts: 0.76 us -> none  [local(): onehot = (prefix_id.reshape(n, rows, 1) == lanes).astype(jnp.bfloat16)]
    broadcast_in_dim x1 -> x0, local copies, waits for them, and re-layouts: 0.73 us -> none  [local(): jnp.broadcast_to(label_cols[:, None, :], (pages, page, HD))]
where the time goes in v1:
time: 49.5 us; the launch traced here: 49.1 us
  Pallas kernels  47.5 us (96%)
  local copies, waits for them, and re-layouts  1.57 us (3%)
    pallas_call x1, Pallas kernels, local(): pl.pallas_call(functools.partial(kernel, n, page), out_shape=jax.ShapeDty...  47.5 us
    unnamed x1, local copies, waits for them, and re-layouts  1.57 us

profile of v1, /device:TPU:0, one launch (start us, length us, event | category | flops | bytes accessed | tf_op | source)
XLA Modules:
  0.0 49.1 jit_solution(16358808331190134882)
XLA Ops:
  0.0 47.5 %step.1 = bf16[16,4096]{1,0:T(8,128)(2,1)} custom-call(bf16[16,4096]{1,0:T(8,128)(2,1)} %q_hbm.1, bf16[16,1024]{1,0:T(8,128)(2,1)} %nk_ref.1, bf16[16,1024]{1,0:T(8,128)(2,1)} %nv_ref.1, bf16[16,256,1024]{2,1,0:T(8,128)(2,1)} %sk_hbm.1, bf16[16,256,1024]{2,1,0:T(8,128)(2,1)} %sv_hbm.1, s32[16]{0:T(128)} %lens_ref.1, bf16[1024,1024]{1,0:T(8,128)(2,1)} %bitcast.3, ...), custom_call_target="tpu_custom_call" | custom-call | tf_op jit(solution)/shard_map/step/pallas_call | solution.py:406
  47.5 1.6 %copy.12 = bf16[16,4096]{1,0:T(8,128)(2,1)} copy(bf16[16,4096]{1,0:T(8,128)(2,1)} %step.1) | data formatting | bytes 262144

commit v2 on v1

v2 whole, which is shorter than its diff:
```python
import functools
import math

import jax
import jax.numpy as jnp
from jax import lax
from jax.experimental import pallas as pl
from jax.experimental.pallas import tpu as pltpu
from jax.sharding import PartitionSpec as P

H = 32
KV = 8
HD = 128
NPREF = 2
G = H // KV
HALF = KV // 2
MASKED = -1e30
SCALE2 = math.log2(math.e) / math.sqrt(HD)
NT = (((1,), (1,)), ((), ()))
MESH = pl.DeviceIdType.MESH


def low_bit(m):
    return m & (-m)


def kernel(
    n, page,
    q_hbm, nk_hbm, nv_hbm, sk_hbm, sv_hbm, lens_ref, pk_hbm, pv_hbm, table_hbm, pid_hbm,
    out_ref,
    nk_ref, nv_ref, table_ref, pid_ref,
    q_own, qs, sk, sv, pk, pv, vt, label, onehot, scores,
    part, lse, near, near_l, fin, got, got_l, cols, cols_got,
    q_rows, nk_rows, nv_rows, home_o, home_l, home_m, weights,
    in_sem, fence, suf_sem, kv_send, kv_recv, ag_send, ag_recv,
    o_send, o_recv, l_send, l_recv, f_send, f_recv,
):
    rows = q_hbm.shape[0]
    slots = sk.shape[1]
    tokens = pk_hbm.shape[0]
    wide_cols = H * HD // 2
    kv_cols = KV * HD // 2
    lanes = 2 * rows * G
    chips = n // 2
    me = lax.axis_index("seq")
    core = me % 2
    chip = me // 2
    other = 1 - core

    def chip_xor(m):
        index = chip
        bit = 1
        while bit < chips:
            if m & bit:
                index = index + bit * (1 - 2 * ((chip // bit) % 2))
            bit *= 2
        return index

    def dev(m, c):
        return chip_xor(m) * 2 + c

    bits = [1 << i for i in range(chips.bit_length() - 1)]
    evens = [m for m in range(2, chips, 2)]
    top_bit = bits[-1]
    middle = bits[1:-1]
    q_paths = (bits[::-1], [top_bit, 1] + middle[::-1])
    o_paths = (None, None) * (HALF // 2)

    def q_hop(m, s):
        return [b for b in q_paths[s] if m & b][-1]

    def o_hop(m, j):
        if o_paths[j] is None:
            return 1 if m % 2 else m
        return [b for b in o_paths[j] if m & b][0]

    def o_children(m, j):
        return [x for x in range(1, chips) if x ^ o_hop(x, j) == m]


    def q_half(h):
        return pl.ds(pl.multiple_of(h * wide_cols, wide_cols), wide_cols)

    def kv_half(h):
        return pl.ds(pl.multiple_of(h * kv_cols, kv_cols), kv_cols)

    def token_half(h):
        return pl.ds(pl.multiple_of(h * tokens, tokens), tokens)

    def remote(src, dst, send, recv, where):
        return pltpu.make_async_remote_copy(
            src_ref=src, dst_ref=dst, send_sem=send, recv_sem=recv,
            device_id={"seq": where}, device_id_type=MESH,
        )

    q_copy = pltpu.make_async_copy(q_hbm, q_own, in_sem.at[0])
    q_mine = pltpu.make_async_copy(q_hbm.at[:, q_half(core)], qs.at[0, core], in_sem.at[1])
    k_mine = pltpu.make_async_copy(
        pk_hbm.at[:, kv_half(core)], pk.at[token_half(core)], in_sem.at[2])
    v_mine = pltpu.make_async_copy(
        pv_hbm.at[:, kv_half(core)], pv.at[token_half(core)], in_sem.at[3])
    small = [
        pltpu.make_async_copy(src, dst, in_sem.at[4 + i])
        for i, (src, dst) in enumerate((
            (nk_hbm, nk_ref), (nv_hbm, nv_ref), (table_hbm, table_ref), (pid_hbm, pid_ref)))
    ]
    q_copy.start()
    q_mine.start()
    for copy in small:
        copy.start()

    def suffix_copies(b):
        return (
            pltpu.make_async_copy(sk_hbm.at[b], sk.at[b], suf_sem.at[0, b]),
            pltpu.make_async_copy(sv_hbm.at[b], sv.at[b], suf_sem.at[1, b]),
        )

    barrier = pltpu.get_barrier_semaphore()
    peers = [dev(0, other)]
    for b in bits:
        peers += [dev(b, 0), dev(b, 1)]
    peers += [dev(m, core) for m in evens if m & (m - 1)]
    for peer in peers:
        pl.semaphore_signal(barrier, inc=1, device_id={"seq": peer}, device_id_type=MESH)
    for b in range(rows // 2):
        for copy in suffix_copies(b):
            copy.start()
    k_mine.start()
    v_mine.start()
    for b in range(rows // 2, rows):
        for copy in suffix_copies(b):
            copy.start()
    pl.semaphore_wait(barrier, len(peers))
    q_copy.wait()

    def own_copy(b, h):
        return remote(
            q_own.at[:, h * wide_cols:(h + 1) * wide_cols], qs.at[b, core],
            ag_send.at[b, h], ag_recv.at[b, core], dev(b, h))

    def forward_copy(m, s):
        hop = q_hop(m, s)
        return remote(
            qs.at[m ^ hop, s], qs.at[m, s], ag_send.at[m, s], ag_recv.at[m, s], dev(hop, core))

    partner_q = remote(
        q_own.at[:, q_half(other)], qs.at[0, core],
        ag_send.at[0, 0], ag_recv.at[0, 0], dev(0, other))
    partner_kv = [
        remote(src.at[:, kv_half(other)], dst.at[token_half(core)],
               kv_send.at[i], kv_recv.at[i], dev(0, other))
        for i, (src, dst) in enumerate(((pk_hbm, pk), (pv_hbm, pv)))
    ]

    for b in bits:
        for h in range(2):
            own_copy(b, h).start()
    partner_q.start()
    for copy in partner_kv:
        copy.start()

    arrived = set([(0, 0), (0, 1)])

    def pull(m, s):
        if (m, s) in arrived:
            return
        arrived.add((m, s))
        hop = q_hop(m, s)
        pull(m ^ hop, s)
        if m == hop:
            remote(
                q_own.at[:, 0:wide_cols], qs.at[m, s],
                ag_send.at[m, s], ag_recv.at[m, s], dev(m, core)).wait_recv()
        else:
            forward_copy(m, s).wait_recv()
        for b in reversed(q_paths[s][q_paths[s].index(hop) + 1:]):
            forward_copy(m | b, s).start()

    def arrive(m):
        for s in range(2):
            pull(m, s)

    for copy in small:
        copy.wait()

    for h in range(H):
        at = pl.ds(h, rows, stride=H)
        k = h // G
        q_rows[at, :] = q_own[:, h * HD:(h + 1) * HD].astype(jnp.float32)
        nk_rows[at, :] = nk_ref[:, k * HD:(k + 1) * HD].astype(jnp.float32)
        nv_rows[at, :] = nv_ref[:, k * HD:(k + 1) * HD].astype(jnp.float32)

    row_head = lax.broadcasted_iota(jnp.int32, (H, HD), 0) // G
    slot_iota = lax.broadcasted_iota(jnp.int32, (H, slots), 1)

    def suffix_scores(b):
        at = slice(b * H, (b + 1) * H)
        q = q_rows[at, :]
        wide = jnp.concatenate(
            [jnp.where(row_head == k, q, 0.0) for k in range(KV)], axis=1
        ).astype(jnp.bfloat16)
        s = lax.dot_general(wide, sk[b], NT, preferred_element_type=jnp.float32)
        s = jnp.where(slot_iota < lens_ref[b], s, MASKED)
        sn = jnp.sum(q * nk_rows[at, :], axis=1, keepdims=True)
        peak = jnp.maximum(jnp.max(s, axis=1, keepdims=True), sn)
        p = jnp.exp2((s - peak) * SCALE2)
        pn = jnp.exp2((sn - peak) * SCALE2)
        mass = jnp.sum(p, axis=1, keepdims=True) + pn
        weights[at, :] = p.astype(jnp.bfloat16)
        home_l[at, :] = jnp.broadcast_to(peak * SCALE2 + jnp.log2(mass), (H, HD))
        home_m[at, :] = jnp.broadcast_to(1.0 / mass, (H, HD))
        home_o[at, :] = pn * nv_rows[at, :]

    def suffix_outputs(b):
        at = slice(b * H, (b + 1) * H)
        o = jnp.dot(weights[at, :], sv[b], preferred_element_type=jnp.float32)
        own = home_o[at, :]
        for k in range(KV):
            own = own + jnp.where(row_head == k, o[:, k * HD:(k + 1) * HD], 0.0)
        home_o[at, :] = own * home_m[at, :]

    def suffix(first, last):
        for b in range(first, last):
            suffix_copies(b)[0].wait()
        for b in range(first, last):
            suffix_scores(b)
        for b in range(first, last):
            suffix_copies(b)[1].wait()
        for b in range(first, last):
            suffix_outputs(b)

    def prepare_labels():
        seqs = n * rows
        diag = (lax.broadcasted_iota(jnp.int32, (seqs, seqs), 0)
                == lax.broadcasted_iota(jnp.int32, (seqs, seqs), 1))
        pid = jnp.sum(jnp.where(diag, pid_ref[...].astype(jnp.float32), 0.0), axis=1, keepdims=True)
        lane = lax.broadcasted_iota(jnp.int32, (seqs, HD), 1).astype(jnp.float32)
        onehot[...] = jnp.where(lane == pid, 1.0, 0.0).astype(jnp.bfloat16)
        pages = 2 * tokens // page
        entries = table_ref.shape[1]
        ids = chip * pages + lax.broadcasted_iota(jnp.int32, (pages, entries), 0)
        page_lane = lax.broadcasted_iota(jnp.int32, (pages, HD), 1)
        bar = jnp.zeros((pages, HD), jnp.float32)
        for p in range(NPREF):
            hit = jnp.max(
                jnp.where(table_ref[p:p + 1, :] == ids, 1.0, 0.0), axis=1, keepdims=True)
            bar = jnp.where(page_lane == p, (1.0 - hit) * MASKED, bar)
        token = lax.broadcasted_iota(jnp.int32, (2 * tokens, pages), 0)
        first = lax.broadcasted_iota(jnp.int32, (2 * tokens, pages), 1) * page
        spread = jnp.where((token >= first) & (token < first + page), 1.0, 0.0)
        label[...] = jnp.dot(
            spread.astype(jnp.bfloat16), bar.astype(jnp.bfloat16),
            preferred_element_type=jnp.float32).astype(jnp.bfloat16)

    def prepare_values():
        v_mine.wait()
        partner_kv[1].wait_recv()
        for k in range(HALF):
            for t in starts:
                vt[k, :HD, t:t + step] = pv[t:t + step, k * HD:(k + 1) * HD].T
            vt[k, HD:, :] = jnp.ones((vt.shape[1] - HD, 2 * tokens), jnp.bfloat16)

    step = 256
    starts = range(0, 2 * tokens, step)

    def query_side(item):
        m, k = item
        parts = [(x, s) for x in (m, m + 1) for s in range(2)]
        code = jnp.concatenate(
            [onehot[pl.ds(pl.multiple_of(dev(x, s) * rows, rows), rows), :]
             for x, s in parts for g in range(G)], axis=0)
        q = jnp.concatenate(
            [qs[x, s, :, (k * G + g) * HD:(k * G + g + 1) * HD]
             for x, s in parts for g in range(G)], axis=0)
        return jnp.concatenate([q, code], axis=1)

    def advance(current, peak, following, slot):
        qx = None if following is None else query_side(following)
        top, o = None, None
        for t in starts:
            at = slice(t, t + step)
            if following is not None:
                k = following[1]
                kx = jnp.concatenate([pk[at, k * HD:(k + 1) * HD], label[at, :]], axis=1)
                s = lax.dot_general(kx, qx, NT, preferred_element_type=jnp.float32)
                scores[1 - slot, at, :] = s
                high = jnp.max(s, axis=0, keepdims=True)
                top = high if top is None else jnp.maximum(top, high)
            if current is not None:
                p = jnp.exp2((scores[slot, at, :] - peak) * SCALE2).astype(jnp.bfloat16)
                d = jnp.dot(vt[current[1], :, at], p, preferred_element_type=jnp.float32)
                o = d if o is None else o + d
        if current is not None:
            m, k = current
            mass = o[HD:HD + 1, :]
            res = (o[:HD, :] * (1.0 / mass)).astype(jnp.bfloat16)
            level = peak * SCALE2 + jnp.log2(mass)
            for x in range(2):
                part[m + x, k] = res[:, x * lanes:(x + 1) * lanes]
                lse[m + x, k] = level[:, x * lanes:(x + 1) * lanes]
        return top

    def part_copies(m, j):
        where = dev(o_hop(m, j), core)
        return [
            remote(part.at[m, j], near.at[m, j], o_send.at[m, j], o_recv.at[m, j], where),
            remote(lse.at[m, j], near_l.at[m, j], l_send.at[m, j], l_recv.at[m, j], where),
        ]

    def merge(m, child, j):
        for copy in part_copies(child, j):
            copy.wait_recv()
        la, lb = near_l[child, j], lse[m, j]
        w = 1.0 / (1.0 + jnp.exp2(lb - la))
        lse[m, j] = jnp.maximum(la, lb) + jnp.log2(1.0 + jnp.exp2(-jnp.abs(la - lb)))
        a = near[child, j].astype(jnp.float32)
        b = part[m, j].astype(jnp.float32)
        part[m, j] = (b + (a - b) * w).astype(jnp.bfloat16)

    def settle(m, j):
        for child in o_children(m, j):
            merge(m, child, j)
        if m:
            for copy in part_copies(m, j):
                copy.start()

    def split():
        pl.semaphore_signal(fence, 1)
        pl.semaphore_wait(fence, 1)

    ready, sent = set(), {}
    clock = [0]

    def depth(node):
        m, j = node
        return 0 if m == 0 else 1 + depth((m ^ o_hop(m, j), j))

    def progress(last):
        lag = 1 if last else 5
        for node in sorted(ready, key=lambda x: (-depth(x), -x[0], x[1])):
            if node[0] == 0 or (node[0] in (1,) and not last):
                continue
            kids = [(c, node[1]) for c in o_children(*node)]
            if all(kid in sent and sent[kid] + lag <= clock[0] for kid in kids):
                settle(*node)
                ready.remove(node)
                sent[node] = clock[0]

    quarter = max(1, rows // 4)
    batches = list(range(0, rows, quarter))

    def fill(count):
        for _ in range(count):
            if batches:
                b = batches.pop(0)
                suffix(b, b + quarter)
                clock[0] += 2

    groups = [0] + evens
    prepare_labels()
    fill(1)
    arrive(groups[1])
    k_mine.wait()
    partner_kv[0].wait_recv()
    q_mine.wait()
    remote(q_own.at[:, 0:wide_cols], qs.at[0, other],
           ag_send.at[0, 0], ag_recv.at[0, 0], dev(0, other)).wait_recv()
    prepare_values()
    for x, m in enumerate(groups):
        if x == len(groups) - 1:
            fill(0)
        arrive(m)
        arrive(m + 1)
        peak = advance(None, None, (m, 0), 1)
        split()
        for k in range(HALF):
            peak = advance((m, k), peak, (m, k + 1) if k + 1 < HALF else None, k % 2)
            split()
            ready |= {(m, k), (m + 1, k)}
            progress(False)
            clock[0] += 1
            if k == 1 and x + 2 < len(groups):
                arrive(groups[x + 2])
    while batches:
        fill(1)
        progress(False)
    while len(sent) < HALF * (chips - 1):
        progress(True)
        clock[0] += 1
    for j in range(HALF):
        settle(0, j)
        fin[j] = part[0, j].astype(jnp.float32).T.astype(jnp.bfloat16)

    def column(src):
        levels = jnp.concatenate([src[k] for k in range(HALF)], axis=0)
        return jnp.concatenate([levels] * (HD // HALF), axis=0).T

    mine = rows * G
    give = remote(
        fin.at[:, pl.ds(pl.multiple_of(other * mine, mine), mine), :], got,
        f_send.at[0], f_recv.at[0], dev(0, other))
    give_l = remote(lse.at[0], got_l, f_send.at[1], f_recv.at[1], dev(0, other))
    give.start()
    give_l.start()

    def finish(half, levels, value):
        for k in range(HALF):
            j, i = k // (HALF // 2), k % (HALF // 2)
            for g in range(G):
                head = half * (HALF * G) + k * G + g
                level = levels[pl.ds(pl.multiple_of(core * mine + g * rows, rows), rows), k:k + 1]
                x = value(k, g).astype(jnp.float32)
                at = pl.ds(head, rows, stride=H)
                home = home_o[at, :]
                w = 1.0 / (1.0 + jnp.exp2(level - home_l[at, :]))
                out_ref[:, pl.ds(pl.multiple_of(head * HD, HD), HD)] = (
                    x + (home - x) * w).astype(jnp.bfloat16)

    cols[...] = column(lse.at[0])
    finish(core, cols, lambda k, g: fin[
        k, pl.ds(pl.multiple_of(core * mine + g * rows, rows), rows), :])
    give.wait_recv()
    give_l.wait_recv()
    cols_got[...] = column(got_l)
    finish(other, cols_got, lambda k, g: got[k, g * rows:(g + 1) * rows, :])

    for b in bits:
        for h in range(2):
            own_copy(b, h).wait_send()
    for m in range(1, chips):
        if m & (m - 1):
            for s in range(2):
                forward_copy(m, s).wait_send()
    partner_q.wait_send()
    for copy in partner_kv:
        copy.wait_send()
    for m in range(1, chips):
        for j in range(HALF):
            for copy in part_copies(m, j):
                copy.wait_send()
    give.wait_send()
    give_l.wait_send()


def local(
    queries, new_keys, new_values, suffix_keys, suffix_values, suffix_lens,
    prefix_keys, prefix_values, page_table, prefix_id,
):
    n = lax.axis_size("seq")
    chips = n // 2
    rows = queries.shape[0]
    slots = suffix_keys.shape[1]
    pages, page, width = prefix_keys.shape
    tokens = pages * page
    vmem = pl.BlockSpec(memory_space=pltpu.VMEM)
    hbm = pl.BlockSpec(memory_space=pl.ANY)
    smem = pl.BlockSpec(memory_space=pltpu.SMEM)
    bf16, f32 = jnp.bfloat16, jnp.float32
    dma = pltpu.SemaphoreType.DMA
    lanes = 2 * rows * G
    return pl.pallas_call(
        functools.partial(kernel, n, page),
        out_shape=jax.ShapeDtypeStruct((rows, H * HD), bf16),
        in_specs=[hbm, hbm, hbm, hbm, hbm, smem, hbm, hbm, hbm, hbm],
        out_specs=vmem,
        scratch_shapes=[
            pltpu.VMEM((rows, width), bf16),
            pltpu.VMEM((rows, width), bf16),
            pltpu.VMEM(page_table.shape, jnp.int32),
            pltpu.VMEM((1, n * rows), jnp.int32),
            pltpu.VMEM((rows, H * HD), bf16),
            pltpu.VMEM((chips, 2, rows, H * HD // 2), bf16),
            pltpu.VMEM((rows, slots, width), bf16),
            pltpu.VMEM((rows, slots, width), bf16),
            pltpu.VMEM((2 * tokens, width // 2), bf16),
            pltpu.VMEM((2 * tokens, width // 2), bf16),
            pltpu.VMEM((HALF, HD + 16, 2 * tokens), bf16),
            pltpu.VMEM((2 * tokens, HD), bf16),
            pltpu.VMEM((n * rows, HD), bf16),
            pltpu.VMEM((2, 2 * tokens, 2 * lanes), f32),
            pltpu.VMEM((chips, HALF, HD, lanes), bf16),
            pltpu.VMEM((chips, HALF, 1, lanes), f32),
            pltpu.VMEM((chips, HALF, HD, lanes), bf16),
            pltpu.VMEM((chips, HALF, 1, lanes), f32),
            pltpu.VMEM((HALF, lanes, HD), bf16),
            pltpu.VMEM((HALF, rows * G, HD), bf16),
            pltpu.VMEM((HALF, 1, lanes), f32),
            pltpu.VMEM((lanes, HD), f32),
            pltpu.VMEM((lanes, HD), f32),
            pltpu.VMEM((rows * H, HD), f32),
            pltpu.VMEM((rows * H, HD), f32),
            pltpu.VMEM((rows * H, HD), f32),
            pltpu.VMEM((rows * H, HD), f32),
            pltpu.VMEM((rows * H, HD), f32),
            pltpu.VMEM((rows * H, HD), f32),
            pltpu.VMEM((rows * H, slots), bf16),
            dma((8,)),
            pltpu.SemaphoreType.REGULAR,
            dma((2, rows)),
            dma((2,)), dma((2,)),
            dma((chips, 2)), dma((chips, 2)),
            dma((chips, HALF)), dma((chips, HALF)), dma((chips, HALF)), dma((chips, HALF)),
            dma((2,)), dma((2,)),
        ],
        compiler_params=pltpu.CompilerParams(
            collective_id=0, has_side_effects=True, vmem_limit_bytes=64 * 1024 * 1024 - 65536,
        ),
        name="step",
    )(
        queries, new_keys, new_values, suffix_keys, suffix_values, suffix_lens,
        prefix_keys.reshape(tokens, width), prefix_values.reshape(tokens, width),
        page_table, prefix_id.reshape(1, n * rows),
    )


def solution(mesh):
    return jax.shard_map(
        local,
        mesh=mesh,
        in_specs=(
            P(("grp", "seq"), None),
            P(("grp", "seq"), None),
            P(("grp", "seq"), None),
            P(("grp", "seq"), None, None),
            P(("grp", "seq"), None, None),
            P(("grp", "seq")),
            P(("grp", "seq"), None, None),
            P(("grp", "seq"), None, None),
            P("grp", None),
            P("grp"),
        ),
        out_specs=P(("grp", "seq"), None),
        check_vma=False,
    )
```

time: 49.5 us -> 44.5 us (0.90)
  Pallas kernels: 47.5 us -> 42.6 us
    pallas_call x1, Pallas kernels: 47.5 us -> 42.6 us  [local(): pl.pallas_call(functools.partial(kernel, n, page), out_shape=jax.ShapeDty...]
where the time goes in v2:
time: 44.5 us; the launch traced here: 44.2 us
  Pallas kernels  42.6 us (96%)
  local copies, waits for them, and re-layouts  1.57 us (4%)
    pallas_call x1, Pallas kernels, local(): pl.pallas_call(functools.partial(kernel, n, page), out_shape=jax.ShapeDty...  42.6 us
    unnamed x1, local copies, waits for them, and re-layouts  1.57 us

profile of v2, /device:TPU:0, one launch (start us, length us, event | category | flops | bytes accessed | tf_op | source)
XLA Modules:
  0.0 44.2 jit_solution(18275184923616245701)
XLA Ops:
  0.0 42.6 %step.1 = bf16[16,4096]{1,0:T(8,128)(2,1)} custom-call(bf16[16,4096]{1,0:T(8,128)(2,1)} %q_hbm.1, bf16[16,1024]{1,0:T(8,128)(2,1)} %nk_hbm.1, bf16[16,1024]{1,0:T(8,128)(2,1)} %nv_hbm.1, bf16[16,256,1024]{2,1,0:T(8,128)(2,1)} %sk_hbm.1, bf16[16,256,1024]{2,1,0:T(8,128)(2,1)} %sv_hbm.1, s32[16]{0:T(128)} %lens_ref.1, bf16[1024,1024]{1,0:T(8,128)(2,1)} %bitcast.3, ...), custom_call_target="tpu_custom_call" | custom-call | tf_op jit(solution)/shard_map/step/pallas_call | solution.py:461
  42.6 1.6 %copy.12 = bf16[16,4096]{1,0:T(8,128)(2,1)} copy(bf16[16,4096]{1,0:T(8,128)(2,1)} %step.1) | data formatting | bytes 262144

commit v3 on v2

--- a/solution.py
+++ b/solution.py
@@ -336,9 +336,9 @@
         return 0 if m == 0 else 1 + depth((m ^ o_hop(m, j), j))
 
     def progress(last):
-        lag = 1 if last else 5
+        lag = 1 if last else 4
         for node in sorted(ready, key=lambda x: (-depth(x), -x[0], x[1])):
-            if node[0] == 0 or (node[0] in (1,) and not last):
+            if node[0] == 0 or (node[0] in () and not last):
                 continue
             kids = [(c, node[1]) for c in o_children(*node)]
             if all(kid in sent and sent[kid] + lag <= clock[0] for kid in kids):
@@ -356,7 +356,7 @@
                 suffix(b, b + quarter)
                 clock[0] += 2
 
-    groups = [0] + evens
+    groups = [0, *evens[1:-1], 2, evens[-1]]
     prepare_labels()
     fill(1)
     arrive(groups[1])

time: 44.5 us -> 41.8 us (0.939)
  Pallas kernels: 42.6 us -> 39.8 us
    pallas_call x1, Pallas kernels: 42.6 us -> 39.8 us  [local(): pl.pallas_call(functools.partial(kernel, n, page), out_shape=jax.ShapeDty...]
where the time goes in v3:
time: 41.8 us; the launch traced here: 41.4 us
  Pallas kernels  39.8 us (95%)
  local copies, waits for them, and re-layouts  1.57 us (4%)
    pallas_call x1, Pallas kernels, local(): pl.pallas_call(functools.partial(kernel, n, page), out_shape=jax.ShapeDty...  39.8 us
    unnamed x1, local copies, waits for them, and re-layouts  1.57 us

profile of v3, /device:TPU:0, one launch (start us, length us, event | category | flops | bytes accessed | tf_op | source)
XLA Modules:
  0.0 41.4 jit_solution(902397570852680297)
XLA Ops:
  0.0 39.8 %step.1 = bf16[16,4096]{1,0:T(8,128)(2,1)} custom-call(bf16[16,4096]{1,0:T(8,128)(2,1)} %q_hbm.1, bf16[16,1024]{1,0:T(8,128)(2,1)} %nk_hbm.1, bf16[16,1024]{1,0:T(8,128)(2,1)} %nv_hbm.1, bf16[16,256,1024]{2,1,0:T(8,128)(2,1)} %sk_hbm.1, bf16[16,256,1024]{2,1,0:T(8,128)(2,1)} %sv_hbm.1, s32[16]{0:T(128)} %lens_ref.1, bf16[1024,1024]{1,0:T(8,128)(2,1)} %bitcast.3, ...), custom_call_target="tpu_custom_call" | custom-call | tf_op jit(solution)/shard_map/step/pallas_call | solution.py:461
  39.9 1.6 %copy.12 = bf16[16,4096]{1,0:T(8,128)(2,1)} copy(bf16[16,4096]{1,0:T(8,128)(2,1)} %step.1) | data formatting | bytes 262144
